TPU v7x, 32 devices: a whole 2x2x4 slice. The times are simulated.
32 devices in a mesh: dp: 8 (over y, x, core), tensor: 4 (over z).
Axes of the slice: x: 2, y: 2, z: 4, core: 2. Of those that a mesh axis runs over, the one named last changes fastest.
Arguments:
- tokens: bfloat16 [8192, 1024], P(('dp', 'tensor')), may hold values from -6 to 6
- block_ids: int32 [8, 1024], P('dp'), may hold values from 0 to 7, never falling along the last dimension, each value on 1 to 256 neighbouring positions
- norm1_gain: bfloat16 [1024], P('dp'), may hold values from 0.25 to 1.75
- q_weight: bfloat16 [1024, 2048], P('dp', 'tensor'), may hold values from -0.1875 to 0.1875
- key_projection: bfloat16 [1024, 1024], P('dp', 'tensor'), may hold values from -0.1875 to 0.1875
- value_projection: bfloat16 [1024, 1024], P('dp', 'tensor'), may hold values from -0.1875 to 0.1875
- q_gain: bfloat16 [128], P('dp'), may hold values from 0.25 to 1.75
- k_gain: bfloat16 [128], P('dp'), may hold values from 0.25 to 1.75
- o_weight: bfloat16 [2048, 1024], P('tensor', 'dp'), may hold values from -2 to 2
- norm2_gain: bfloat16 [1024], P('dp'), may hold values from 0.25 to 1.75
- gate_weight: bfloat16 [1024, 3072], P('dp', 'tensor'), may hold values from -0.1875 to 0.1875
- up_weight: bfloat16 [1024, 3072], P('dp', 'tensor'), may hold values from -0.1875 to 0.1875
- down_weight: bfloat16 [3072, 1024], P('tensor', 'dp'), may hold values from -0.109375 to 0.109375
- out_grad: bfloat16 [8192, 1024], P(('dp', 'tensor')), may hold values from -6 to 6
Outputs:
- layer_out: bfloat16 [8192, 1024], P(('dp', 'tensor'))
- tokens_grad: float32 [8192, 1024], P(('dp', 'tensor'))
- norm1_grad: float32 [1024], P('dp')
- q_weight_grad: float32 [1024, 2048], P('dp', 'tensor')
- k_weight_grad: float32 [1024, 1024], P('dp', 'tensor')
- v_weight_grad: float32 [1024, 1024], P('dp', 'tensor')
- q_gain_grad: float32 [128], P('dp')
- k_gain_grad: float32 [128], P('dp')
- o_weight_grad: float32 [2048, 1024], P('tensor', 'dp')
- norm2_grad: float32 [1024], P('dp')
- gate_weight_grad: float32 [1024, 3072], P('dp', 'tensor')
- up_weight_grad: float32 [1024, 3072], P('dp', 'tensor')
- down_weight_grad: float32 [3072, 1024], P('tensor', 'dp')
Inputs may be any that keep to these rules, and one draw needn't show every extreme that they name: `block_ids`: in each row block numbers never fall and every number from the least to the largest is used; each block has 1 to 256 tokens and some block has exactly 256.
All inputs are finite; a program needn't handle non-finite values.
Results may differ from a plain program's by a relative error of at most 0.017.
Values may be sent and summed in bfloat16 or wider, within the bound.
A program may use at most 128 MiB of HBM per device.

v0:
```python
from functools import partial
import jax
import jax.numpy as jnp
from jax import lax
from jax.sharding import PartitionSpec as P

EPSILON = 1e-06
BASE_FREQ = 1000000.0
MASKED = -1e30


def rms_scale(values, gain):
    return values * lax.rsqrt(jnp.mean(values * values, axis=-1, keepdims=True) + EPSILON) * gain


def rotate(values, cosine, sine):
    half = values.shape[-1] // 2
    turned = jnp.concatenate([-values[..., half:], values[..., :half]], axis=-1)
    return values * cosine + turned * sine


def angles(sequence_length, width):
    half = width // 2
    inverse = BASE_FREQ ** (-2.0 * jnp.arange(half, dtype=jnp.float32) / width)
    places = jnp.arange(sequence_length, dtype=jnp.float32)
    turns = places[:, None] * inverse[None, :]
    turns = jnp.concatenate([turns, turns], axis=-1)
    return (jnp.cos(turns)[:, None, :], jnp.sin(turns)[:, None, :])


def shape_heads(raw, gain, cosine, sine):
    return rotate(rms_scale(raw, gain), cosine, sine)


def contract_rows(left, right):
    return lax.dot_general(
        left, right, (((0,), (0,)), ((), ())), preferred_element_type=jnp.float32
    )


def contract_cols(left, right):
    return lax.dot_general(
        left, right, (((1,), (1,)), ((), ())), preferred_element_type=jnp.float32
    )


def attend_forward(queries_rot, keys_rot, rotated_values, block_of):
    sequence_length, heads, width = queries_rot.shape
    kv_heads = keys_rot.shape[1]
    head_group = heads // kv_heads
    extent_size = min(512, sequence_length)
    count = sequence_length // extent_size
    scale = width ** (-0.5)

    def one_block(inputs):
        query_block_index, block_rows = inputs
        grouped_heads = query_block_index.reshape(extent_size, kv_heads, head_group, width)
        scores = (
            jnp.einsum(
                "qhgd,khd->hgqk", grouped_heads, keys_rot, preferred_element_type=jnp.float32
            )
            * scale
        )
        seen = block_of[None, :] <= block_rows[:, None]
        scores = jnp.where(seen, scores, MASKED)
        highest = jnp.max(scores, axis=-1, keepdims=True)
        raised = jnp.exp(scores - highest)
        totals = jnp.sum(raised, axis=-1, keepdims=True)
        weights = (raised / totals).astype(jnp.bfloat16)
        mixed = jnp.einsum(
            "hgqk,khd->qhgd", weights, rotated_values, preferred_element_type=jnp.float32
        )
        return (
            mixed.reshape(extent_size, heads * width),
            highest[..., 0] + jnp.log(totals[..., 0]),
        )

    mixed, log_totals = lax.map(
        one_block,
        (
            queries_rot.reshape(count, extent_size, heads, width),
            block_of.reshape(count, extent_size),
        ),
    )
    return (mixed.reshape(sequence_length, heads * width), log_totals)


def attend_backward(queries_rot, keys_rot, rotated_values, block_of, log_totals, mixed_grad):
    sequence_length, heads, width = queries_rot.shape
    kv_heads = keys_rot.shape[1]
    head_group = heads // kv_heads
    extent_size = min(512, sequence_length)
    count = sequence_length // extent_size
    scale = width ** (-0.5)

    def one_block(carry, inputs):
        key_acc, value_acc = carry
        query_block_index, block_rows, log_block, grad_block = inputs
        grouped_heads = query_block_index.reshape(extent_size, kv_heads, head_group, width)
        grad_grouped = grad_block.reshape(extent_size, kv_heads, head_group, width)
        scores = (
            jnp.einsum(
                "qhgd,khd->hgqk", grouped_heads, keys_rot, preferred_element_type=jnp.float32
            )
            * scale
        )
        seen = block_of[None, :] <= block_rows[:, None]
        scores = jnp.where(seen, scores, MASKED)
        weights = jnp.exp(scores - log_block[..., None])
        weight_grad = jnp.einsum(
            "qhgd,khd->hgqk", grad_grouped, rotated_values, preferred_element_type=jnp.float32
        )
        centre = jnp.sum(weights * weight_grad, axis=-1, keepdims=True)
        score_grad = (weights * (weight_grad - centre)).astype(jnp.bfloat16)
        query_grad = (
            jnp.einsum("hgqk,khd->qhgd", score_grad, keys_rot, preferred_element_type=jnp.float32)
            * scale
        )
        key_acc = (
            key_acc
            + jnp.einsum(
                "hgqk,qhgd->khd", score_grad, grouped_heads, preferred_element_type=jnp.float32
            )
            * scale
        )
        value_acc = value_acc + jnp.einsum(
            "hgqk,qhgd->khd",
            weights.astype(jnp.bfloat16),
            grad_grouped,
            preferred_element_type=jnp.float32,
        )
        return ((key_acc, value_acc), query_grad.reshape(extent_size, heads * width))

    zeros = jnp.zeros((sequence_length, kv_heads, width), jnp.float32)
    (key_grad, value_grad), query_grad = lax.scan(
        one_block,
        (zeros, zeros),
        (
            queries_rot.reshape(count, extent_size, heads, width),
            block_of.reshape(count, extent_size),
            log_totals,
            mixed_grad.reshape(count, extent_size, heads, width),
        ),
    )
    return (query_grad.reshape(sequence_length, heads, width), key_grad, value_grad)


def body(
    tokens,
    block_ids,
    norm1_gain,
    q_weight,
    key_projection,
    value_projection,
    q_gain,
    k_gain,
    o_weight,
    norm2_gain,
    gate_weight,
    up_weight,
    down_weight,
    out_grad,
):
    shards = (
        norm1_gain,
        q_weight,
        key_projection,
        value_projection,
        q_gain,
        k_gain,
        o_weight,
        norm2_gain,
        gate_weight,
        up_weight,
        down_weight,
    )
    gathered = (
        lax.all_gather(shards[0], "dp", axis=0, tiled=True),
        lax.all_gather(shards[1], "dp", axis=0, tiled=True),
        lax.all_gather(shards[2], "dp", axis=0, tiled=True),
        lax.all_gather(shards[3], "dp", axis=0, tiled=True),
        lax.all_gather(shards[4], "dp", axis=0, tiled=True),
        lax.all_gather(shards[5], "dp", axis=0, tiled=True),
        lax.all_gather(shards[6], "dp", axis=1, tiled=True),
        lax.all_gather(shards[7], "dp", axis=0, tiled=True),
        lax.all_gather(shards[8], "dp", axis=0, tiled=True),
        lax.all_gather(shards[9], "dp", axis=0, tiled=True),
        lax.all_gather(shards[10], "dp", axis=1, tiled=True),
    )
    (
        gain_first,
        q_mat,
        key_matrix,
        value_matrix,
        q_scale,
        k_scale,
        o_mat,
        gain_second,
        gate_mat,
        up_mat,
        down_mat,
    ) = gathered
    block_of = block_ids[0]
    sequence_length = block_of.shape[0]
    head_dim = q_scale.shape[0]
    q_cols = q_weight.shape[1]
    kv_cols = key_projection.shape[1]
    ff_local = gate_weight.shape[1]
    heads = q_cols // head_dim
    kv_heads = kv_cols // head_dim
    cosine, sine = angles(sequence_length, head_dim)
    acts = tokens.astype(jnp.float32)
    first_gain = gain_first.astype(jnp.float32)
    second_gain = gain_second.astype(jnp.float32)
    qkv_mat = jnp.concatenate([q_mat, key_matrix, value_matrix], axis=1)
    gate_up = jnp.concatenate([gate_mat, up_mat], axis=1)
    normed_own = rms_scale(acts, first_gain).astype(jnp.bfloat16)
    piece = lax.all_gather(normed_own, "tensor", axis=0, tiled=True)
    projected = jnp.dot(piece, qkv_mat, preferred_element_type=jnp.float32)
    normalized_input = piece
    q_raw = projected[:, :q_cols].reshape(sequence_length, heads, head_dim)
    key_unrotated = projected[:, q_cols : q_cols + kv_cols].reshape(
        sequence_length, kv_heads, head_dim
    )
    rotated_values = (
        projected[:, q_cols + kv_cols :]
        .astype(jnp.bfloat16)
        .reshape(sequence_length, kv_heads, head_dim)
    )
    head_shaper = partial(shape_heads, cosine=cosine, sine=sine)
    q_shaped, q_pull = jax.vjp(head_shaper, q_raw, q_scale.astype(jnp.float32))
    k_shaped, k_pull = jax.vjp(head_shaper, key_unrotated, k_scale.astype(jnp.float32))
    queries_rot = q_shaped.astype(jnp.bfloat16)
    keys_rot = k_shaped.astype(jnp.bfloat16)
    mixed_full, log_totals = attend_forward(queries_rot, keys_rot, rotated_values, block_of)
    mixed = mixed_full.astype(jnp.bfloat16)
    state = acts + lax.psum_scatter(
        jnp.dot(mixed, o_mat, preferred_element_type=jnp.float32),
        "tensor",
        scatter_dimension=0,
        tiled=True,
    )
    normed_two_own = rms_scale(state, second_gain).astype(jnp.bfloat16)
    piece = lax.all_gather(normed_two_own, "tensor", axis=0, tiled=True)
    gate_both = jnp.dot(piece, gate_up, preferred_element_type=jnp.float32)
    normed_two = piece
    gate_pre = gate_both[:, :ff_local]
    up_pre = gate_both[:, ff_local:]
    sigmoid_gate = jax.nn.sigmoid(gate_pre)
    silu_gate = gate_pre * sigmoid_gate
    inner = (silu_gate * up_pre).astype(jnp.bfloat16)
    layer_sum = state + lax.psum_scatter(
        jnp.dot(inner, down_mat, preferred_element_type=jnp.float32).astype(jnp.bfloat16),
        "tensor",
        scatter_dimension=0,
        tiled=True,
    ).astype(jnp.float32)
    layer_out = layer_sum.astype(jnp.bfloat16)
    gathered = (
        lax.all_gather(shards[0], "dp", axis=0, tiled=True),
        lax.all_gather(shards[1], "dp", axis=0, tiled=True),
        lax.all_gather(shards[2], "dp", axis=0, tiled=True),
        lax.all_gather(shards[3], "dp", axis=0, tiled=True),
        lax.all_gather(shards[4], "dp", axis=0, tiled=True),
        lax.all_gather(shards[5], "dp", axis=0, tiled=True),
        lax.all_gather(shards[6], "dp", axis=1, tiled=True),
        lax.all_gather(shards[7], "dp", axis=0, tiled=True),
        lax.all_gather(shards[8], "dp", axis=0, tiled=True),
        lax.all_gather(shards[9], "dp", axis=0, tiled=True),
        lax.all_gather(shards[10], "dp", axis=1, tiled=True),
    )
    (
        gain_first,
        q_mat,
        key_matrix,
        value_matrix,
        q_scale,
        k_scale,
        o_mat,
        gain_second,
        gate_mat,
        up_mat,
        down_mat,
    ) = gathered
    qkv_mat = jnp.concatenate([q_mat, key_matrix, value_matrix], axis=1)
    gate_up = jnp.concatenate([gate_mat, up_mat], axis=1)
    piece = lax.all_gather(out_grad, "tensor", axis=0, tiled=True)
    inner_grad = contract_cols(piece, down_mat)
    grad_full = piece
    down_grad = contract_rows(inner, grad_full)
    gate_grad = inner_grad * up_pre * sigmoid_gate * (1.0 + gate_pre * (1.0 - sigmoid_gate))
    up_grad = inner_grad * silu_gate
    gate_up_grad = jnp.concatenate([gate_grad, up_grad], axis=1).astype(jnp.bfloat16)
    gate_up_wgrad = contract_rows(normed_two, gate_up_grad)
    normed_two_grad = lax.psum_scatter(
        contract_cols(gate_up_grad, gate_up).astype(jnp.bfloat16),
        "tensor",
        scatter_dimension=0,
        tiled=True,
    ).astype(jnp.float32)
    second_pull = jax.vjp(rms_scale, state, second_gain)[1]
    state_back, second_part = second_pull(normed_two_grad)
    state_grad = out_grad.astype(jnp.float32) + state_back
    piece = lax.all_gather(state_grad.astype(jnp.bfloat16), "tensor", axis=0, tiled=True)
    mixed_grad = contract_cols(piece, o_mat)
    o_grad = contract_rows(mixed, piece)
    q_rot_grad, k_rot_grad, v_grad = attend_backward(
        queries_rot, keys_rot, rotated_values, block_of, log_totals, mixed_grad.astype(jnp.bfloat16)
    )
    q_raw_grad, q_part = q_pull(q_rot_grad)
    k_raw_grad, k_part = k_pull(k_rot_grad)
    qkv_grad = jnp.concatenate(
        [
            q_raw_grad.reshape(sequence_length, q_cols),
            k_raw_grad.reshape(sequence_length, kv_cols),
            v_grad.reshape(sequence_length, kv_cols),
        ],
        axis=1,
    ).astype(jnp.bfloat16)
    qkv_wgrad = contract_rows(normalized_input, qkv_grad)
    normed_grad = lax.psum_scatter(
        contract_cols(qkv_grad, qkv_mat).astype(jnp.bfloat16),
        "tensor",
        scatter_dimension=0,
        tiled=True,
    ).astype(jnp.float32)
    first_pull = jax.vjp(rms_scale, acts, first_gain)[1]
    acts_back, first_part = first_pull(normed_grad)
    tokens_grad = state_grad + acts_back
    q_wgrad = qkv_wgrad[:, :q_cols]
    k_wgrad = qkv_wgrad[:, q_cols : q_cols + kv_cols]
    v_wgrad = qkv_wgrad[:, q_cols + kv_cols :]
    (
        first_sum,
        q_sum,
        k_sum,
        v_sum,
        qs_sum,
        ks_sum,
        o_sum,
        second_sum,
        gate_sum,
        up_sum,
        down_sum,
    ) = (
        lax.psum_scatter(first_part, "dp", scatter_dimension=0, tiled=True),
        lax.psum_scatter(q_wgrad, "dp", scatter_dimension=0, tiled=True),
        lax.psum_scatter(k_wgrad, "dp", scatter_dimension=0, tiled=True),
        lax.psum_scatter(v_wgrad, "dp", scatter_dimension=0, tiled=True),
        lax.psum_scatter(q_part, "dp", scatter_dimension=0, tiled=True),
        lax.psum_scatter(k_part, "dp", scatter_dimension=0, tiled=True),
        lax.psum_scatter(o_grad, "dp", scatter_dimension=1, tiled=True),
        lax.psum_scatter(second_part, "dp", scatter_dimension=0, tiled=True),
        lax.psum_scatter(gate_up_wgrad[:, :ff_local], "dp", scatter_dimension=0, tiled=True),
        lax.psum_scatter(gate_up_wgrad[:, ff_local:], "dp", scatter_dimension=0, tiled=True),
        lax.psum_scatter(down_grad, "dp", scatter_dimension=1, tiled=True),
    )
    first_total, second_total, qs_total, ks_total = lax.psum(
        (first_sum, second_sum, qs_sum, ks_sum), "tensor"
    )
    return (
        layer_out,
        tokens_grad,
        first_total,
        q_sum,
        k_sum,
        v_sum,
        qs_total,
        ks_total,
        o_sum,
        second_total,
        gate_sum,
        up_sum,
        down_sum,
    )


def solution(mesh):
    return jax.shard_map(
        body,
        mesh=mesh,
        in_specs=(
            P(("dp", "tensor"), None),
            P("dp", None),
            P("dp"),
            P("dp", "tensor"),
            P("dp", "tensor"),
            P("dp", "tensor"),
            P("dp"),
            P("dp"),
            P("tensor", "dp"),
            P("dp"),
            P("dp", "tensor"),
            P("dp", "tensor"),
            P("tensor", "dp"),
            P(("dp", "tensor"), None),
        ),
        out_specs=(
            P(("dp", "tensor"), None),
            P(("dp", "tensor"), None),
            P("dp"),
            P("dp", "tensor"),
            P("dp", "tensor"),
            P("dp", "tensor"),
            P("dp"),
            P("dp"),
            P("tensor", "dp"),
            P("dp"),
            P("dp", "tensor"),
            P("dp", "tensor"),
            P("tensor", "dp"),
        ),
        check_vma=False,
    )
```

profile of v0, /device:TPU:0, one launch (start us, length us, event | category | flops | bytes accessed | tf_op | source)
XLA Modules:
  0.0 1014.9 jit_solution(3832472821615925314)
XLA Ops:
  8.0 10.4 %all-gather = bf16[8,1,128]{2,1,0:T(2,128)(2,1)S(1)} all-gather(bf16[1,1,128]{2,1,0:T(2,128)(2,1)} %bitcast.258), channel_id=1, replica_groups=mesh['dp'=8,'tensor'=4] {'dp'}, dimensions={0}, use_global_device_ids=true | all-gather | bytes 2304 | tf_op jit(solution)/shard_map/all_gather | solution.py:178
  22.6 9.7 all_gather.55
  32.4 9.0 all_gather.56
  43.1 13.8 %all-reduce.12 = (bf16[128]{0:T(256)(128)(2,1)S(1)}, bf16[128]{0:T(256)(128)(2,1)S(1)}) all-reduce(bf16[128]{0:T(256)(128)(2,1)S(1)} %dynamic-update-slice, bf16[128]{0:T(256)(128)(2,1)S(1)} %dynamic-update-slice.1), channel_id=1, replica_groups=mesh['dp'=8,'tensor'=4] {'dp'}, use_global_device_ids=true, to_apply=%add.4 | all-reduce | flops 256 | bytes 1024
  57.0 2.6 fusion.56
  59.7 9.1 fusion.58
  74.1 9.8 all-gather.12.cloned.1.call-done
  83.9 4.6 fusion.73
  96.8 3.1 concatenate.44
  99.9 3.1 concatenate.45
  103.0 2.8 reshape.258
  105.8 4.5 fusion.35
  110.2 2.6 copy.108
  112.9 20.0 %while.27 = (s32[]{:T(128)}, bf16[2,512,512]{2,1,0:T(8,128)(2,1)}, f32[2,2,2,512]{3,2,1,0:T(2,128)S(1)}, s32[1,1024]{1,0:T(1,128)S(1)}, s32[2,512]{1,0:T(2,128)S...) while((s32[]{:T(128)}, bf16[2,512,512]{2,1,0:T(8,128)(2,1)}, ...), condition=%wide.region_6.7_spmd, body=%wide.region_3.6_spmd.sunk | while | flops 1099429888 | bytes 32582248 | solution.py:78
  113.5 2.8 bitcast_reduce_fusion.2
  118.8 3.1 fusion.126
  123.4 2.8 bitcast_reduce_fusion.2
  128.6 3.1 fusion.126
  132.8 5.2 fusion.74
  139.3 8.7 all-gather.1
  148.0 65.8 %reduce-scatter.12.cloned.1.call-done = f32[256,1024]{1,0:T(8,128)} async-done(((f32[1024,1024]{1,0:T(8,128)}), f32[256,1024]{1,0:T(8,128)}) %reduce-scatter.12.cloned.1.call-update) | async-done | bytes 1048592 | tf_op jit(solution)/shard_map/reduce_scatter | solution.py:237
  217.9 23.7 %all-gather.20.cloned.1.call-done = bf16[1024,768]{1,0:T(8,128)(2,1)} async-done(((bf16[128,768]{1,0:T(8,128)(2,1)}), bf16[1024,768]{1,0:T(8,128)(2,1)}) %all-gather.20.cloned.1.call-update) | async-done | bytes 1572880 | tf_op jit(solution)/shard_map/all_gather | solution.py:186
  241.7 2.8 constant_dynamic-update-slice_fusion.5
  244.4 24.6 %all-gather.22.cloned.1.call-done = bf16[1024,768]{1,0:T(8,128)(2,1)} async-done(((bf16[128,768]{1,0:T(8,128)(2,1)}), bf16[1024,768]{1,0:T(8,128)(2,1)}) %all-gather.22.cloned.1.call-update) | async-done | bytes 1572880 | tf_op jit(solution)/shard_map/all_gather | solution.py:187
  269.0 2.7 constant_dynamic-update-slice_fusion.4
  271.7 45.1 %all-gather.18.cloned.1.call-done = bf16[1024,1024]{1,0:T(8,128)(2,1)} async-done(((bf16[256,1024]{1,0:T(8,128)(2,1)}), bf16[1024,1024]{1,0:T(8,128)(2,1)}) %all-gather.18.cloned.1.call-update) | async-done | bytes 2097168 | tf_op jit(solution)/shard_map/all_gather | solution.py:244
  316.8 8.6 fusion.75
  325.4 17.9 %all-gather.24.cloned.1.call-done = bf16[768,1024]{1,0:T(8,128)(2,1)} async-done(((bf16[768,128]{1,0:T(8,128)(2,1)}), bf16[768,1024]{1,0:T(8,128)(2,1)}) %all-gather.24.cloned.1.call-update) | async-done | bytes 1572880 | tf_op jit(solution)/shard_map/all_gather | solution.py:188
  343.3 47.3 %all-gather.26.cloned.1.call-done = bf16[1024,1024]{1,0:T(8,128)(2,1)} async-done(((bf16[256,1024]{1,0:T(8,128)(2,1)}), bf16[1024,1024]{1,0:T(8,128)(2,1)}) %all-gather.26.cloned.1.call-update) | async-done | bytes 2097168 | tf_op jit(solution)/shard_map/all_gather | solution.py:287
  390.6 8.0 multiply_convert_fusion.1
  400.2 4.7 fusion.38
  405.4 42.1 %reduce-scatter.16.cloned.1.call-done = bf16[256,1024]{1,0:T(8,128)(2,1)} async-done(((bf16[1024,1024]{1,0:T(8,128)(2,1)}), bf16[256,1024]{1,0:T(8,128)(2,1)}) %reduce-scatter.16.cloned.1.call-update) | async-done | bytes 524304 | tf_op jit(solution)/shard_map/reduce_scatter | solution.py:295
  453.1 43.6 %all-gather.28.cloned.1.call-done = bf16[1024,1024]{1,0:T(8,128)(2,1)} async-done(((bf16[256,1024]{1,0:T(8,128)(2,1)}), bf16[1024,1024]{1,0:T(8,128)(2,1)}) %all-gather.28.cloned.1.call-update) | async-done | bytes 2097168 | tf_op jit(solution)/shard_map/all_gather | solution.py:304
  496.7 3.1 convolution_convert_fusion.2
  501.0 81.2 %while.28 = (s32[]{:T(128)}, f32[1024,2,128]{0,2,1:T(8,128)S(1)}, f32[1024,2,128]{0,2,1:T(8,128)}, f32[2,512,512]{1,0,2:T(2,128)}, bf16[2,512,4,128]{3,1,2,0:T(8...) while((s32[]{:T(128)}, f32[1024,2,128]{0,2,1:T(8,128)S(1)}, ...), condition=%wide.region_14.15_spmd.clone, body=%wide.region_12.14_spmd.clone.sunk | while | flops 2717906944 | bytes 181995984 | solution.py:135
  504.4 3.4 fusion.137
  513.2 19.5 %dynamic_update_slice.19 = f32[2,512,512]{1,0,2:T(2,128)} dynamic-update-slice(f32[2,512,512]{1,0,2:T(2,128)} %get-tuple-element.505, f32[1,512,512]{1,0,2:T(1,128)S(1)} %copy.162, s32[]{:T(128)} %get-tuple-element.502, s32[]{:T(128)} %constant.43.clone.1..sunk, s32[]{:T(128)} %constant.43.clone.1..sunk) | dynamic-update-slice | bytes 2097156 | tf_op jit(solution)/shard_map/while/body/jit(dynamic_update_index_in_dim)/dynamic_update_slice | solution.py:78
  532.7 3.3 fusion.139
  537.4 3.6 fusion.140
  544.5 3.4 fusion.137
  553.3 19.5 %dynamic_update_slice.19 = f32[2,512,512]{1,0,2:T(2,128)} dynamic-update-slice(f32[2,512,512]{1,0,2:T(2,128)} %get-tuple-element.505, f32[1,512,512]{1,0,2:T(1,128)S(1)} %copy.162, s32[]{:T(128)} %get-tuple-element.502, s32[]{:T(128)} %constant.43.clone.1..sunk, s32[]{:T(128)} %constant.43.clone.1..sunk) | dynamic-update-slice | bytes 2097156 | tf_op jit(solution)/shard_map/while/body/jit(dynamic_update_index_in_dim)/dynamic_update_slice | solution.py:78
  572.8 3.3 fusion.139
  577.5 4.7 fusion.140
  582.2 4.2 reshape.296
  596.5 5.3 convolution_convert_fusion
  603.2 4.5 convolution_convert_fusion.1
  609.4 5.4 fusion.36
  614.8 3.3 fusion.68
  619.7 5.0 fusion.77
  625.9 4.0 fusion.54
  634.1 2.6 fusion.76
  636.8 3.1 slice.66
  641.4 3.0 reduce-scatter.18.cloned.1.call-done
  646.0 14.1 %all-reduce.10 = (f32[1024]{0:T(1024)S(1)}, f32[128]{0:T(128)S(1)}, f32[128]{0:T(128)S(1)}, f32[1024]{0:T(1024)S(1)}) all-reduce(f32[1024]{0:T(1024)S(1)} %get-tuple-element.257, f32[128]{0:T(128)S(1)} %get-tuple-element.251, f32[128]{0:T(128)S(1)} %get-tuple-element.255, ...), channel_id=6, replica_groups=mesh['dp'=8,'tensor'=4] {'dp'}, use_global_device_ids=true, to_apply=%region_20.21.clone | all-reduce | flops 2304 | bytes 18432
  660.4 11.4 %all-reduce.11 = (f32[128]{0:T(128)}, f32[16]{0:T(128)}, f32[16]{0:T(128)}, f32[128]{0:T(128)}) all-reduce(f32[128]{0:T(128)S(1)} %dynamic-slice.3, f32[16]{0:T(128)S(1)} %dynamic-slice.5, f32[16]{0:T(128)S(1)} %dynamic-slice.7, f32[128]{0:T(128)S(1)} %dynamic-slice.9), channel_id=1, replica_groups=mesh['dp'=8,'tensor'=4] {'tensor'}, use_global_device_ids=true, to_apply=%region_21.22 | all-reduce | flops 288 | bytes 2304 | tf_op jit(solution)/shard_map/psum | solution.py:358
  671.8 18.0 %reduce-scatter.14.cloned.1.call-done = bf16[256,1024]{1,0:T(8,128)(2,1)} async-done(((bf16[1024,1024]{1,0:T(8,128)(2,1)}), bf16[256,1024]{1,0:T(8,128)(2,1)}) %reduce-scatter.14.cloned.1.call-update) | async-done | bytes 524304 | tf_op jit(solution)/shard_map/reduce_scatter | solution.py:252
  689.9 2.9 fusion.49
  692.8 46.2 %reduce-scatter.28.cloned.1.call-done = f32[128,768]{1,0:T(8,128)} async-done(((f32[1024,768]{1,0:T(8,128)}), f32[128,768]{1,0:T(8,128)}) %reduce-scatter.28.cloned.1.call-update) | async-done | bytes 393232 | tf_op jit(solution)/shard_map/reduce_scatter | solution.py:354
  739.0 49.9 %reduce-scatter.30.cloned.1.call-done = f32[128,768]{1,0:T(8,128)} async-done(((f32[1024,768]{1,0:T(8,128)}), f32[128,768]{1,0:T(8,128)}) %reduce-scatter.30.cloned.1.call-update) | async-done | bytes 393232 | tf_op jit(solution)/shard_map/reduce_scatter | solution.py:355
  788.9 49.9 %reduce-scatter.32.cloned.1.call-done = f32[768,128]{1,0:T(8,128)} async-done(((f32[768,1024]{1,0:T(8,128)}), f32[768,128]{1,0:T(8,128)}) %reduce-scatter.32.cloned.1.call-update) | async-done | bytes 393232 | tf_op jit(solution)/shard_map/reduce_scatter | solution.py:356
  838.8 39.6 %reduce-scatter.22.cloned.1.call-done = f32[128,256]{1,0:T(8,128)} async-done(((f32[1024,256]{1,0:T(8,128)}), f32[128,256]{1,0:T(8,128)}) %reduce-scatter.22.cloned.1.call-update) | async-done | bytes 131088 | tf_op jit(solution)/shard_map/reduce_scatter | solution.py:348
  878.4 39.6 %reduce-scatter.24.cloned.1.call-done = f32[128,256]{1,0:T(8,128)} async-done(((f32[1024,256]{1,0:T(8,128)}), f32[128,256]{1,0:T(8,128)}) %reduce-scatter.24.cloned.1.call-update) | async-done | bytes 131088 | tf_op jit(solution)/shard_map/reduce_scatter | solution.py:349
  918.0 45.0 %reduce-scatter.26.cloned.1.call-done = f32[512,128]{1,0:T(8,128)} async-done(((f32[512,1024]{1,0:T(8,128)}), f32[512,128]{1,0:T(8,128)}) %reduce-scatter.26.cloned.1.call-update) | async-done | bytes 262160 | tf_op jit(solution)/shard_map/reduce_scatter | solution.py:352
  963.0 44.9 %reduce-scatter.20.cloned.1.call-done = f32[128,512]{1,0:T(8,128)} async-done(((f32[1024,512]{1,0:T(8,128)}), f32[128,512]{1,0:T(8,128)}) %reduce-scatter.20.cloned.1.call-update) | async-done | bytes 262160 | tf_op jit(solution)/shard_map/reduce_scatter | solution.py:347
  (314 shorter events, 83.3 us)
Async XLA Ops:
  7.2 34.2 %copy-start.68 = (u32[32]{0:T(128)S(1)}, u32[32]{0:T(128)}, u32[]{:S(2)}) copy-start(u32[32]{0:T(128)} %constant.90) | copy-start | bytes 388
  7.2 15.4 %copy-start.51 = (bf16[128,256]{1,0:T(8,128)(2,1)S(1)}, bf16[128,256]{1,0:T(8,128)(2,1)}, u32[]{:S(2)}) copy-start(bf16[128,256]{1,0:T(8,128)(2,1)} %param.22) | copy-start | bytes 196612
  7.2 25.2 %copy-start.52 = (bf16[128,256]{1,0:T(8,128)(2,1)S(1)}, bf16[128,256]{1,0:T(8,128)(2,1)}, u32[]{:S(2)}) copy-start(bf16[128,256]{1,0:T(8,128)(2,1)} %param.23) | copy-start | bytes 196612
  7.2 35.4 %copy-start.71 = (bf16[16]{0:T(256)(128)(2,1)S(1)}, bf16[16]{0:T(256)(128)(2,1)}, u32[]{:S(2)}) copy-start(bf16[16]{0:T(256)(128)(2,1)} %param.24) | copy-start | bytes 100
  7.2 35.7 %copy-start.72 = (bf16[16]{0:T(256)(128)(2,1)S(1)}, bf16[16]{0:T(256)(128)(2,1)}, u32[]{:S(2)}) copy-start(bf16[16]{0:T(256)(128)(2,1)} %param.25) | copy-start | bytes 100
  7.2 62.8 %all-gather.14.cloned.1.call-start = ((), (), s32[]{:S(2)}) async-start(), calls=%async_computation.12 | async-start | bytes 1179648 | tf_op jit(solution)/shard_map/all_gather | solution.py:179
  8.0 75.9 %all-gather.12.cloned.1.call-start = ((), (), s32[]{:S(2)}) async-start(), calls=%async_computation.11 | async-start | bytes 2621440 | tf_op jit(solution)/shard_map/all_gather | solution.py:218
  18.4 4.2 copy-start.53
  21.7 111.1 %all-gather.16.cloned.1.call-start = ((), (), s32[]{:S(2)}) async-start(), calls=%async_computation.13 | async-start | bytes 1179648 | tf_op jit(solution)/shard_map/all_gather | solution.py:184
  22.5 191.3 %reduce-scatter.12.cloned.1.call-start = ((), (), s32[]{:S(2)}) async-start(), calls=%async_computation.14 | async-start | bytes 5242880 | tf_op jit(solution)/shard_map/reduce_scatter | solution.py:237
  22.6 46.7 %copy-start.40 = (s32[1,1024]{1,0:T(1,128)S(1)}, s32[1,1024]{1,0:T(1,128)}, u32[]{:S(2)}) copy-start(s32[1,1024]{1,0:T(1,128)} %param.19) | copy-start | bytes 12292
  56.9 34.0 %copy-start.66 = (f32[128]{0:T(128)}, f32[128]{0:T(128)S(1)}, u32[]{:S(2)}) copy-start(f32[128]{0:T(128)S(1)} %convert_element_type.84) | copy-start | bytes 1540
  59.6 31.3 %copy-start.20 = (f32[1024,128]{0,1:T(8,128)}, f32[1024,128]{0,1:T(8,128)S(1)}, u32[]{:S(2)}) copy-start(f32[1024,128]{0,1:T(8,128)S(1)} %get-tuple-element.332) | copy-start | bytes 1572868
  59.6 46.2 %copy-start.64 = (f32[128]{0:T(128)}, f32[128]{0:T(128)S(1)}, u32[]{:S(2)}) copy-start(f32[128]{0:T(128)S(1)} %convert_element_type.82) | copy-start | bytes 1540
  88.9 4.4 copy-start.45
  89.1 13.8 %copy-start.14 = (f32[1024,512]{0,1:T(8,128)}, f32[1024,512]{0,1:T(8,128)S(1)}, u32[]{:S(2)}) copy-start(f32[1024,512]{0,1:T(8,128)S(1)} %slice.57) | copy-start | bytes 6291460
  132.8 5.2 copy-start.9
  138.0 75.8 %copy-start.17 = (bf16[256,1024]{1,0:T(8,128)(2,1)S(1)}, bf16[256,1024]{1,0:T(8,128)(2,1)}, u32[]{:S(2)}) copy-start(bf16[256,1024]{1,0:T(8,128)(2,1)} %param.18) | copy-start | bytes 1572868
  138.0 103.6 %all-gather.20.cloned.1.call-start = ((), (), s32[]{:S(2)}) async-start(), calls=%async_computation.16 | async-start | bytes 1769472 | tf_op jit(solution)/shard_map/all_gather | solution.py:186
  138.6 130.4 %all-gather.22.cloned.1.call-start = ((), (), s32[]{:S(2)}) async-start(), calls=%async_computation.17 | async-start | bytes 1769472 | tf_op jit(solution)/shard_map/all_gather | solution.py:187
  139.2 177.6 %all-gather.18.cloned.1.call-start = ((), (), s32[]{:S(2)}) async-start(), calls=%async_computation.15 | async-start | bytes 2621440 | tf_op jit(solution)/shard_map/all_gather | solution.py:244
  148.0 301.5 %copy-start.47 = (f32[8,1,128]{2,1,0:T(1,128)}, f32[8,1,128]{2,1,0:T(1,128)S(1)}, u32[]{:S(2)}) copy-start(f32[8,1,128]{2,1,0:T(1,128)S(1)} %convert_element_type.102) | copy-start | bytes 12292
  215.3 234.2 %copy-start.10 = (f32[256,1024]{1,0:T(8,128)}, f32[256,1024]{1,0:T(8,128)S(1)}, u32[]{:S(2)}) copy-start(f32[256,1024]{1,0:T(8,128)S(1)} %get-tuple-element.310) | copy-start | bytes 3145732
  215.3 234.2 %copy-start.55 = (f32[256]{0:T(256)}, f32[256]{0:T(256)S(1)}, u32[]{:S(2)}) copy-start(f32[256]{0:T(256)S(1)} %fusion.62) | copy-start | bytes 3076
  216.4 126.9 %all-gather.24.cloned.1.call-start = ((), (), s32[]{:S(2)}) async-start(), calls=%async_computation.18 | async-start | bytes 1769472 | tf_op jit(solution)/shard_map/all_gather | solution.py:188
  217.1 173.4 %all-gather.26.cloned.1.call-start = ((), (), s32[]{:S(2)}) async-start(), calls=%async_computation.20 | async-start | bytes 2621440 | tf_op jit(solution)/shard_map/all_gather | solution.py:287
  217.9 229.6 %reduce-scatter.16.cloned.1.call-start = ((), (), s32[]{:S(2)}) async-start(), calls=%async_computation.21 | async-start | bytes 2621440 | tf_op jit(solution)/shard_map/reduce_scatter | solution.py:295
  390.6 9.6 copy-start.35
  404.9 44.6 %copy-start.24 = (bf16[256,1024]{1,0:T(8,128)(2,1)S(1)}, bf16[256,1024]{1,0:T(8,128)(2,1)}, u32[]{:S(2)}) copy-start(bf16[256,1024]{1,0:T(8,128)(2,1)} %param.31) | copy-start | bytes 1572868
  404.9 91.8 %all-gather.28.cloned.1.call-start = ((), (), s32[]{:S(2)}) async-start(), calls=%async_computation.22 | async-start | bytes 2621440 | tf_op jit(solution)/shard_map/all_gather | solution.py:304
  449.5 3.6 copy-start.60
  451.7 192.7 %reduce-scatter.18.cloned.1.call-start = ((), (), s32[]{:S(2)}) async-start(), calls=%async_computation.23 | async-start | bytes 2621440 | tf_op jit(solution)/shard_map/reduce_scatter | solution.py:321
  501.0 9.2 copy-start.3
  503.7 4.1 copy-start
  532.7 4.6 copy-start.1
  532.7 4.7 copy-start.8
  537.4 3.6 copy-start.13
  541.0 9.3 copy-start.3
  543.8 4.1 copy-start
  572.8 4.6 copy-start.1
  572.8 4.7 copy-start.8
  577.5 4.7 copy-start.4
  577.5 4.7 copy-start.13
  582.2 4.3 copy-start.23
  582.2 6.6 copy-start.42
  601.9 88.0 %reduce-scatter.14.cloned.1.call-start = ((), (), s32[]{:S(2)}) async-start(), calls=%async_computation.19 | async-start | bytes 2621440 | tf_op jit(solution)/shard_map/reduce_scatter | solution.py:252
  607.8 131.2 %reduce-scatter.28.cloned.1.call-start = ((), (), s32[]{:S(2)}) async-start(), calls=%async_computation.28 | async-start | bytes 3538944 | tf_op jit(solution)/shard_map/reduce_scatter | solution.py:354
  618.1 170.8 %reduce-scatter.30.cloned.1.call-start = ((), (), s32[]{:S(2)}) async-start(), calls=%async_computation.29 | async-start | bytes 3538944 | tf_op jit(solution)/shard_map/reduce_scatter | solution.py:355
  618.7 220.1 %reduce-scatter.32.cloned.1.call-start = ((), (), s32[]{:S(2)}) async-start(), calls=%async_computation.30 | async-start | bytes 3538944 | tf_op jit(solution)/shard_map/reduce_scatter | solution.py:356
  624.7 253.7 %reduce-scatter.22.cloned.1.call-start = ((), (), s32[]{:S(2)}) async-start(), calls=%async_computation.25 | async-start | bytes 1179648 | tf_op jit(solution)/shard_map/reduce_scatter | solution.py:348
  632.5 285.4 %reduce-scatter.24.cloned.1.call-start = ((), (), s32[]{:S(2)}) async-start(), calls=%async_computation.26 | async-start | bytes 1179648 | tf_op jit(solution)/shard_map/reduce_scatter | solution.py:349
  633.1 329.9 %reduce-scatter.26.cloned.1.call-start = ((), (), s32[]{:S(2)}) async-start(), calls=%async_computation.27 | async-start | bytes 2359296 | tf_op jit(solution)/shard_map/reduce_scatter | solution.py:352
  636.7 371.1 %reduce-scatter.20.cloned.1.call-start = ((), (), s32[]{:S(2)}) async-start(), calls=%async_computation.24 | async-start | bytes 2359296 | tf_op jit(solution)/shard_map/reduce_scatter | solution.py:347
  636.8 7.7 copy-start.54
  636.8 7.7 copy-start.59
  639.9 4.5 copy-start.18
  639.9 6.1 copy-start.57
  639.9 31.9 %copy-start.63 = (f32[256]{0:T(256)S(1)}, f32[256]{0:T(256)}, u32[]{:S(2)}) copy-start(f32[256]{0:T(256)} %copy-done.62) | copy-start | bytes 3076
  639.9 50.0 %copy-start.11 = (f32[256,1024]{1,0:T(8,128)S(1)}, f32[256,1024]{1,0:T(8,128)}, u32[]{:S(2)}) copy-start(f32[256,1024]{1,0:T(8,128)} %copy-done.10) | copy-start | bytes 3145732
  639.9 50.0 %copy-start.25 = (bf16[256,1024]{1,0:T(8,128)(2,1)S(1)}, bf16[256,1024]{1,0:T(8,128)(2,1)}, u32[]{:S(2)}) copy-start(bf16[256,1024]{1,0:T(8,128)(2,1)} %param.31) | copy-start | bytes 1572868
  639.9 49.9 %copy-start.26 = (bf16[256,1024]{1,0:T(8,128)(2,1)S(1)}, bf16[256,1024]{1,0:T(8,128)(2,1)}, u32[]{:S(2)}) copy-start(bf16[256,1024]{1,0:T(8,128)(2,1)} %reduce-scatter.16.cloned.1.call-done) | copy-start | bytes 1572868
  639.9 49.9 %copy-start.48 = (f32[8,1,128]{2,1,0:T(1,128)S(1)}, f32[8,1,128]{2,1,0:T(1,128)}, u32[]{:S(2)}) copy-start(f32[8,1,128]{2,1,0:T(1,128)} %copy-done.47) | copy-start | bytes 12292
  640.0 49.9 %copy-start.56 = (f32[256]{0:T(256)S(1)}, f32[256]{0:T(256)}, u32[]{:S(2)}) copy-start(f32[256]{0:T(256)} %copy-done.55) | copy-start | bytes 3076
  640.0 49.9 %copy-start.61 = (f32[256]{0:T(256)S(1)}, f32[256]{0:T(256)}, u32[]{:S(2)}) copy-start(f32[256]{0:T(256)} %copy-done.60) | copy-start | bytes 3076
  (42 other events, 84.1 us)
Sparse Core Ops, SparseCore 0:
  9.9 26.0 all-gather.13
  38.2 45.6 all-gather.11
  85.8 22.2 all-gather.15
  138.1 75.6 reduce-scatter.11
  215.5 26.0 all-gather.19
  243.4 25.5 all-gather.21
  271.1 45.6 all-gather.17
  318.7 24.5 all-gather.23
  344.9 45.6 all-gather.25
  405.1 42.3 reduce-scatter.15
  451.8 44.8 all-gather.27
  602.0 42.4 reduce-scatter.17
  646.7 43.0 reduce-scatter.13
  693.7 45.2 reduce-scatter.27
  742.8 46.0 reduce-scatter.29
  792.7 46.0 reduce-scatter.31
  842.4 35.9 reduce-scatter.21
  882.0 35.9 reduce-scatter.23
  921.8 41.1 reduce-scatter.25
  966.7 41.1 reduce-scatter.19
where the time goes:
time: 1020 us; the launch traced here: 1010 us
  waiting for transfers between devices  661 us (65%)
  local copies, waits for them, and re-layouts  105 us (10%)
  matrix products  100 us (10%)
  blocking collectives  77.2 us (8%)
  other arithmetic  52.2 us (5%)
  between operations  17.5 us (2%)
    reduce_scatter x1, waiting for transfers between devices, body(): lax.psum_scatter(jnp.dot(mixed, o_mat, preferred_element_type=jnp.float32...  65.8 us
    reduce_scatter x1, waiting for transfers between devices, body(): lax.psum_scatter(down_grad, 'dp', scatter_dimension=1, tiled=True)  49.9 us
    reduce_scatter x1, waiting for transfers between devices, body(): lax.psum_scatter(gate_up_wgrad[:, ff_local:], 'dp', scatter_dimension=0,...  49.9 us
    all_gather x1, waiting for transfers between devices, body(): piece = lax.all_gather(out_grad, 'tensor', axis=0, tiled=True)  47.3 us
    reduce_scatter x1, waiting for transfers between devices, body(): lax.psum_scatter(gate_up_wgrad[:, :ff_local], 'dp', scatter_dimension=0,...  46.2 us
    all_gather x1, waiting for transfers between devices, body(): piece = lax.all_gather(normed_two_own, 'tensor', axis=0, tiled=True)  45.1 us
    reduce_scatter x1, waiting for transfers between devices, body(): lax.psum_scatter(o_grad, 'dp', scatter_dimension=1, tiled=True)  45 us
    reduce_scatter x1, waiting for transfers between devices, body(): lax.psum_scatter(q_wgrad, 'dp', scatter_dimension=0, tiled=True)  44.9 us
  transfers between devices with their start and end apart: 20, of which 18 were waited for; matrix products, arithmetic and copies ran while one was open for 12% of the time, Pallas kernels for 0%

commit v1 on v0

--- a/solution.py
+++ b/solution.py
@@ -241,7 +241,18 @@
         tiled=True,
     )
     normed_two_own = rms_scale(state, second_gain).astype(jnp.bfloat16)
-    piece = lax.all_gather(normed_two_own, "tensor", axis=0, tiled=True)
+    now = lax.axis_size("tensor")
+    response = lax.axis_index("tensor")
+    heard, arr_now = (now, response)
+    piece, next_value = (normed_two_own, 1)
+    while next_value < heard:
+        d_next = lax.ppermute(
+            piece, axis_name="tensor", perm=[(j, j ^ next_value) for j in range(heard)]
+        )
+        r1 = jnp.concatenate([piece, d_next], 0)
+        passed = jnp.concatenate([d_next, piece], 0)
+        piece = jnp.where(arr_now & next_value == 0, r1, passed)
+        next_value = 2 * next_value
     gate_both = jnp.dot(piece, gate_up, preferred_element_type=jnp.float32)
     normed_two = piece
     gate_pre = gate_both[:, :ff_local]

time: 1020 us -> 975 us (0.956)
  waiting for transfers between devices: 661 us -> 609 us
    all_gather x1 -> x0, waiting for transfers between devices: 45.1 us -> none  [body(): piece = lax.all_gather(normed_two_own, 'tensor', axis=0, tiled=True)]
    ppermute x0 -> x2, waiting for transfers between devices: none -> 18.7 us  [body(): lax.ppermute(piece, axis_name='tensor', perm=[(j, j ^ next_value) for j i...]
    all_gather x1, waiting for transfers between devices: 23.7 us -> 8.14 us  [body(): lax.all_gather(shards[8], 'dp', axis=0, tiled=True)]
    unnamed x144 -> x146, local copies, waits for them, and re-layouts: 22.5 us -> 22.1 us
  transfers between devices with their start and end apart: 20 -> 21, of which waited for: 18 -> 19; matrix products, arithmetic and copies ran while one was open for 12% -> 13% of each run, Pallas kernels for 0% -> 0%
where the time goes in v1:
time: 975 us; the launch traced here: 968 us
  waiting for transfers between devices  609 us (62%)
  local copies, waits for them, and re-layouts  104 us (11%)
  matrix products  102 us (10%)
  blocking collectives  77.1 us (8%)
  other arithmetic  52.7 us (5%)
  between operations  17.2 us (2%)
    reduce_scatter x1, waiting for transfers between devices, body(): lax.psum_scatter(jnp.dot(mixed, o_mat, preferred_element_type=jnp.float32...  64.3 us
    reduce_scatter x1, waiting for transfers between devices, body(): lax.psum_scatter(gate_up_wgrad[:, ff_local:], 'dp', scatter_dimension=0,...  49.9 us
    reduce_scatter x1, waiting for transfers between devices, body(): lax.psum_scatter(down_grad, 'dp', scatter_dimension=1, tiled=True)  49.9 us
    all_gather x1, waiting for transfers between devices, body(): piece = lax.all_gather(out_grad, 'tensor', axis=0, tiled=True)  47.3 us
    reduce_scatter x1, waiting for transfers between devices, body(): lax.psum_scatter(gate_up_wgrad[:, :ff_local], 'dp', scatter_dimension=0,...  46.3 us
    reduce_scatter x1, waiting for transfers between devices, body(): lax.psum_scatter(q_wgrad, 'dp', scatter_dimension=0, tiled=True)  45 us
    reduce_scatter x1, waiting for transfers between devices, body(): lax.psum_scatter(o_grad, 'dp', scatter_dimension=1, tiled=True)  44.8 us
    all_gather x1, waiting for transfers between devices, body(): lax.all_gather(state_grad.astype(jnp.bfloat16), 'tensor', axis=0, tiled=T...  43.6 us
  transfers between devices with their start and end apart: 21, of which 19 were waited for; matrix products, arithmetic and copies ran while one was open for 13% of the time, Pallas kernels for 0%

profile of v1, /device:TPU:0, one launch (start us, length us, event | category | flops | bytes accessed | tf_op | source)
XLA Modules:
  0.0 968.2 jit_solution(11750981052881513641)
XLA Ops:
  8.0 10.4 %all-gather = bf16[8,1,128]{2,1,0:T(2,128)(2,1)S(1)} all-gather(bf16[1,1,128]{2,1,0:T(2,128)(2,1)} %bitcast.256), channel_id=1, replica_groups=mesh['dp'=8,'tensor'=4] {'dp'}, dimensions={0}, use_global_device_ids=true | all-gather | bytes 2304 | tf_op jit(solution)/shard_map/all_gather | solution.py:178
  22.6 9.7 %all_gather.52 = bf16[1024,256]{1,0:T(8,128)(2,1)S(1)} all-gather(bf16[128,256]{1,0:T(8,128)(2,1)S(1)} %copy-done.51), channel_id=1, replica_groups=mesh['dp'=8,'tensor'=4] {'dp'}, dimensions={0}, use_global_device_ids=true | all-gather | bytes 589824 | tf_op jit(solution)/shard_map/all_gather | solution.py:180
  32.4 9.0 all_gather.53
  43.1 13.8 %all-reduce.12 = (bf16[128]{0:T(256)(128)(2,1)S(1)}, bf16[128]{0:T(256)(128)(2,1)S(1)}) all-reduce(bf16[128]{0:T(256)(128)(2,1)S(1)} %dynamic-update-slice, bf16[128]{0:T(256)(128)(2,1)S(1)} %dynamic-update-slice.1), channel_id=1, replica_groups=mesh['dp'=8,'tensor'=4] {'dp'}, use_global_device_ids=true, to_apply=%add.4 | all-reduce | flops 256 | bytes 1024
  59.7 9.1 fusion.59
  74.1 9.8 %all-gather.11.cloned.1.call-done = bf16[1024,1024]{1,0:T(8,128)(2,1)} async-done(((bf16[256,1024]{1,0:T(8,128)(2,1)}), bf16[1024,1024]{1,0:T(8,128)(2,1)}) %all-gather.11.cloned.1.call-update) | async-done | bytes 2097168 | tf_op jit(solution)/shard_map/all_gather | solution.py:218
  83.9 4.6 fusion.75
  96.8 3.1 concatenate.56
  99.9 3.1 concatenate.57
  103.0 2.8 reshape.258
  105.8 4.5 fusion.35
  112.9 20.0 %while.27 = (s32[]{:T(128)}, bf16[2,512,512]{2,1,0:T(8,128)(2,1)}, f32[2,2,2,512]{3,2,1,0:T(2,128)S(1)}, s32[1,1024]{1,0:T(1,128)S(1)}, s32[2,512]{1,0:T(2,128)S...) while((s32[]{:T(128)}, bf16[2,512,512]{2,1,0:T(8,128)(2,1)}, ...), condition=%wide.region_6.7_spmd, body=%wide.region_3.6_spmd.sunk | while | flops 1099429888 | bytes 32582248 | solution.py:78
  113.5 2.8 bitcast_reduce_fusion.2
  118.8 3.1 fusion.125
  123.4 2.8 bitcast_reduce_fusion.2
  128.6 3.1 fusion.125
  132.8 5.2 fusion.76
  140.8 8.7 all-gather.1
  149.5 64.3 %reduce-scatter.12.cloned.1.call-done = f32[256,1024]{1,0:T(8,128)} async-done(((f32[1024,1024]{1,0:T(8,128)}), f32[256,1024]{1,0:T(8,128)}) %reduce-scatter.12.cloned.1.call-update) | async-done | bytes 1048592 | tf_op jit(solution)/shard_map/reduce_scatter | solution.py:237
  217.0 11.9 %collective-permute-done = bf16[256,1024]{1,0:T(8,128)(2,1)S(1)} collective-permute-done((bf16[256,1024]{1,0:T(8,128)(2,1)S(1)}, bf16[256,1024]{1,0:T(8,128)(2,1)S(1)}, u32[]{:S(2)}, u32[]{:S(2)}) %collective-permute-start) | collective-permute-done | bytes 524320 | tf_op jit(solution)/shard_map/ppermute | solution.py:249
  230.3 3.2 collective-permute-start.1
  233.5 8.1 all-gather.17.cloned.1.call-done
  241.7 2.8 constant_dynamic-update-slice_fusion.5
  244.4 24.6 %all-gather.19.cloned.1.call-done = bf16[1024,768]{1,0:T(8,128)(2,1)} async-done(((bf16[128,768]{1,0:T(8,128)(2,1)}), bf16[1024,768]{1,0:T(8,128)(2,1)}) %all-gather.19.cloned.1.call-update) | async-done | bytes 1572880 | tf_op jit(solution)/shard_map/all_gather | solution.py:187
  269.0 2.7 constant_dynamic-update-slice_fusion.4
  271.7 6.9 collective-permute-done.1
  278.5 9.0 fusion.57
  287.5 9.2 all-gather.21.cloned.1.call-done
  296.7 47.3 %all-gather.23.cloned.1.call-done = bf16[1024,1024]{1,0:T(8,128)(2,1)} async-done(((bf16[256,1024]{1,0:T(8,128)(2,1)}), bf16[1024,1024]{1,0:T(8,128)(2,1)}) %all-gather.23.cloned.1.call-update) | async-done | bytes 2097168 | tf_op jit(solution)/shard_map/all_gather | solution.py:298
  343.9 8.0 multiply_convert_fusion.1
  353.6 5.1 fusion.38
  358.7 42.5 %reduce-scatter.16.cloned.1.call-done = bf16[256,1024]{1,0:T(8,128)(2,1)} async-done(((bf16[1024,1024]{1,0:T(8,128)(2,1)}), bf16[256,1024]{1,0:T(8,128)(2,1)}) %reduce-scatter.16.cloned.1.call-update) | async-done | bytes 524304 | tf_op jit(solution)/shard_map/reduce_scatter | solution.py:306
  406.9 43.6 %all-gather.25.cloned.1.call-done = bf16[1024,1024]{1,0:T(8,128)(2,1)} async-done(((bf16[256,1024]{1,0:T(8,128)(2,1)}), bf16[1024,1024]{1,0:T(8,128)(2,1)}) %all-gather.25.cloned.1.call-update) | async-done | bytes 2097168 | tf_op jit(solution)/shard_map/all_gather | solution.py:315
  450.5 3.1 convolution_convert_fusion.2
  454.7 81.2 %while.28 = (s32[]{:T(128)}, f32[1024,2,128]{0,2,1:T(8,128)S(1)}, f32[1024,2,128]{0,2,1:T(8,128)}, f32[2,512,512]{1,0,2:T(2,128)}, bf16[2,512,4,128]{3,1,2,0:T(8...) while((s32[]{:T(128)}, f32[1024,2,128]{0,2,1:T(8,128)S(1)}, ...), condition=%wide.region_14.15_spmd.clone, body=%wide.region_12.14_spmd.clone.sunk | while | flops 2717906944 | bytes 181995984 | solution.py:135
  458.1 3.4 fusion.136
  467.0 19.5 %dynamic_update_slice.19 = f32[2,512,512]{1,0,2:T(2,128)} dynamic-update-slice(f32[2,512,512]{1,0,2:T(2,128)} %get-tuple-element.505, f32[1,512,512]{1,0,2:T(1,128)S(1)} %copy.162, s32[]{:T(128)} %get-tuple-element.502, s32[]{:T(128)} %constant.44.clone.1..sunk, s32[]{:T(128)} %constant.44.clone.1..sunk) | dynamic-update-slice | bytes 2097156 | tf_op jit(solution)/shard_map/while/body/jit(dynamic_update_index_in_dim)/dynamic_update_slice | solution.py:78
  486.4 3.3 fusion.138
  491.1 3.6 fusion.139
  498.2 3.4 fusion.136
  507.0 19.5 %dynamic_update_slice.19 = f32[2,512,512]{1,0,2:T(2,128)} dynamic-update-slice(f32[2,512,512]{1,0,2:T(2,128)} %get-tuple-element.505, f32[1,512,512]{1,0,2:T(1,128)S(1)} %copy.162, s32[]{:T(128)} %get-tuple-element.502, s32[]{:T(128)} %constant.44.clone.1..sunk, s32[]{:T(128)} %constant.44.clone.1..sunk) | dynamic-update-slice | bytes 2097156 | tf_op jit(solution)/shard_map/while/body/jit(dynamic_update_index_in_dim)/dynamic_update_slice | solution.py:78
  526.5 3.3 fusion.138
  531.2 4.7 fusion.139
  535.9 4.2 reshape.296
  550.2 5.3 convolution_convert_fusion
  556.9 4.5 convolution_convert_fusion.1
  562.7 6.1 fusion.36
  568.8 3.3 fusion.70
  573.7 5.0 fusion.78
  579.9 4.0 fusion.54
  588.1 2.6 fusion.77
  590.8 3.1 slice.66
  595.5 2.7 reduce-scatter.18.cloned.1.call-done
  599.7 14.1 %all-reduce.10 = (f32[1024]{0:T(1024)S(1)}, f32[128]{0:T(128)S(1)}, f32[128]{0:T(128)S(1)}, f32[1024]{0:T(1024)S(1)}) all-reduce(f32[1024]{0:T(1024)S(1)} %get-tuple-element.257, f32[128]{0:T(128)S(1)} %get-tuple-element.251, f32[128]{0:T(128)S(1)} %get-tuple-element.255, ...), channel_id=6, replica_groups=mesh['dp'=8,'tensor'=4] {'dp'}, use_global_device_ids=true, to_apply=%region_20.21.clone | all-reduce | flops 2304 | bytes 18432
  614.1 11.3 %all-reduce.11 = (f32[128]{0:T(128)}, f32[16]{0:T(128)}, f32[16]{0:T(128)}, f32[128]{0:T(128)}) all-reduce(f32[128]{0:T(128)S(1)} %dynamic-slice.3, f32[16]{0:T(128)S(1)} %dynamic-slice.5, f32[16]{0:T(128)S(1)} %dynamic-slice.7, f32[128]{0:T(128)S(1)} %dynamic-slice.9), channel_id=1, replica_groups=mesh['dp'=8,'tensor'=4] {'tensor'}, use_global_device_ids=true, to_apply=%region_21.22 | all-reduce | flops 288 | bytes 2304 | tf_op jit(solution)/shard_map/psum | solution.py:369
  625.4 18.0 %reduce-scatter.14.cloned.1.call-done = bf16[256,1024]{1,0:T(8,128)(2,1)} async-done(((bf16[1024,1024]{1,0:T(8,128)(2,1)}), bf16[256,1024]{1,0:T(8,128)(2,1)}) %reduce-scatter.14.cloned.1.call-update) | async-done | bytes 524304 | tf_op jit(solution)/shard_map/reduce_scatter | solution.py:263
  643.4 2.9 fusion.49
  646.3 46.3 %reduce-scatter.28.cloned.1.call-done = f32[128,768]{1,0:T(8,128)} async-done(((f32[1024,768]{1,0:T(8,128)}), f32[128,768]{1,0:T(8,128)}) %reduce-scatter.28.cloned.1.call-update) | async-done | bytes 393232 | tf_op jit(solution)/shard_map/reduce_scatter | solution.py:365
  692.6 49.9 %reduce-scatter.30.cloned.1.call-done = f32[128,768]{1,0:T(8,128)} async-done(((f32[1024,768]{1,0:T(8,128)}), f32[128,768]{1,0:T(8,128)}) %reduce-scatter.30.cloned.1.call-update) | async-done | bytes 393232 | tf_op jit(solution)/shard_map/reduce_scatter | solution.py:366
  742.5 49.9 %reduce-scatter.32.cloned.1.call-done = f32[768,128]{1,0:T(8,128)} async-done(((f32[768,1024]{1,0:T(8,128)}), f32[768,128]{1,0:T(8,128)}) %reduce-scatter.32.cloned.1.call-update) | async-done | bytes 393232 | tf_op jit(solution)/shard_map/reduce_scatter | solution.py:367
  792.4 39.6 %reduce-scatter.22.cloned.1.call-done = f32[128,256]{1,0:T(8,128)} async-done(((f32[1024,256]{1,0:T(8,128)}), f32[128,256]{1,0:T(8,128)}) %reduce-scatter.22.cloned.1.call-update) | async-done | bytes 131088 | tf_op jit(solution)/shard_map/reduce_scatter | solution.py:359
  832.1 39.6 %reduce-scatter.24.cloned.1.call-done = f32[128,256]{1,0:T(8,128)} async-done(((f32[1024,256]{1,0:T(8,128)}), f32[128,256]{1,0:T(8,128)}) %reduce-scatter.24.cloned.1.call-update) | async-done | bytes 131088 | tf_op jit(solution)/shard_map/reduce_scatter | solution.py:360
  871.7 44.8 %reduce-scatter.26.cloned.1.call-done = f32[512,128]{1,0:T(8,128)} async-done(((f32[512,1024]{1,0:T(8,128)}), f32[512,128]{1,0:T(8,128)}) %reduce-scatter.26.cloned.1.call-update) | async-done | bytes 262160 | tf_op jit(solution)/shard_map/reduce_scatter | solution.py:363
  916.5 45.0 %reduce-scatter.20.cloned.1.call-done = f32[128,512]{1,0:T(8,128)} async-done(((f32[1024,512]{1,0:T(8,128)}), f32[128,512]{1,0:T(8,128)}) %reduce-scatter.20.cloned.1.call-update) | async-done | bytes 262160 | tf_op jit(solution)/shard_map/reduce_scatter | solution.py:358
  (318 shorter events, 89.7 us)
Async XLA Ops:
  7.2 34.2 %copy-start.68 = (u32[32]{0:T(128)S(1)}, u32[32]{0:T(128)}, u32[]{:S(2)}) copy-start(u32[32]{0:T(128)} %constant.98) | copy-start | bytes 388
  7.2 15.4 %copy-start.51 = (bf16[128,256]{1,0:T(8,128)(2,1)S(1)}, bf16[128,256]{1,0:T(8,128)(2,1)}, u32[]{:S(2)}) copy-start(bf16[128,256]{1,0:T(8,128)(2,1)} %param.22) | copy-start | bytes 196612
  7.2 25.2 %copy-start.52 = (bf16[128,256]{1,0:T(8,128)(2,1)S(1)}, bf16[128,256]{1,0:T(8,128)(2,1)}, u32[]{:S(2)}) copy-start(bf16[128,256]{1,0:T(8,128)(2,1)} %param.23) | copy-start | bytes 196612
  7.2 35.4 %copy-start.72 = (bf16[16]{0:T(256)(128)(2,1)S(1)}, bf16[16]{0:T(256)(128)(2,1)}, u32[]{:S(2)}) copy-start(bf16[16]{0:T(256)(128)(2,1)} %param.24) | copy-start | bytes 100
  7.2 35.7 %copy-start.73 = (bf16[16]{0:T(256)(128)(2,1)S(1)}, bf16[16]{0:T(256)(128)(2,1)}, u32[]{:S(2)}) copy-start(bf16[16]{0:T(256)(128)(2,1)} %param.25) | copy-start | bytes 100
  7.2 62.8 %all-gather.13.cloned.1.call-start = ((), (), s32[]{:S(2)}) async-start(), calls=%async_computation.12 | async-start | bytes 1179648 | tf_op jit(solution)/shard_map/all_gather | solution.py:179
  8.0 75.9 %all-gather.11.cloned.1.call-start = ((), (), s32[]{:S(2)}) async-start(), calls=%async_computation.11 | async-start | bytes 2621440 | tf_op jit(solution)/shard_map/all_gather | solution.py:218
  18.4 4.2 copy-start.53
  21.7 111.1 %all-gather.15.cloned.1.call-start = ((), (), s32[]{:S(2)}) async-start(), calls=%async_computation.13 | async-start | bytes 1179648 | tf_op jit(solution)/shard_map/all_gather | solution.py:184
  22.5 191.3 %reduce-scatter.12.cloned.1.call-start = ((), (), s32[]{:S(2)}) async-start(), calls=%async_computation.14 | async-start | bytes 5242880 | tf_op jit(solution)/shard_map/reduce_scatter | solution.py:237
  22.6 46.7 %copy-start.40 = (s32[1,1024]{1,0:T(1,128)S(1)}, s32[1,1024]{1,0:T(1,128)}, u32[]{:S(2)}) copy-start(s32[1,1024]{1,0:T(1,128)} %param.19) | copy-start | bytes 12292
  56.9 34.0 %copy-start.66 = (f32[128]{0:T(128)}, f32[128]{0:T(128)S(1)}, u32[]{:S(2)}) copy-start(f32[128]{0:T(128)S(1)} %convert_element_type.84) | copy-start | bytes 1540
  59.6 31.3 %copy-start.20 = (f32[1024,128]{0,1:T(8,128)}, f32[1024,128]{0,1:T(8,128)S(1)}, u32[]{:S(2)}) copy-start(f32[1024,128]{0,1:T(8,128)S(1)} %get-tuple-element.332) | copy-start | bytes 1572868
  59.6 46.2 %copy-start.64 = (f32[128]{0:T(128)}, f32[128]{0:T(128)S(1)}, u32[]{:S(2)}) copy-start(f32[128]{0:T(128)S(1)} %convert_element_type.82) | copy-start | bytes 1540
  88.9 4.4 copy-start.45
  89.1 13.8 %copy-start.14 = (f32[1024,512]{0,1:T(8,128)}, f32[1024,512]{0,1:T(8,128)S(1)}, u32[]{:S(2)}) copy-start(f32[1024,512]{0,1:T(8,128)S(1)} %slice.57) | copy-start | bytes 6291460
  132.8 5.2 copy-start.9
  138.0 75.8 %copy-start.17 = (bf16[256,1024]{1,0:T(8,128)(2,1)S(1)}, bf16[256,1024]{1,0:T(8,128)(2,1)}, u32[]{:S(2)}) copy-start(bf16[256,1024]{1,0:T(8,128)(2,1)} %param.18) | copy-start | bytes 1572868
  138.0 103.6 %all-gather.17.cloned.1.call-start = ((), (), s32[]{:S(2)}) async-start(), calls=%async_computation.15 | async-start | bytes 1769472 | tf_op jit(solution)/shard_map/all_gather | solution.py:186
  138.6 130.4 %all-gather.19.cloned.1.call-start = ((), (), s32[]{:S(2)}) async-start(), calls=%async_computation.16 | async-start | bytes 1769472 | tf_op jit(solution)/shard_map/all_gather | solution.py:187
  139.2 157.5 %all-gather.21.cloned.1.call-start = ((), (), s32[]{:S(2)}) async-start(), calls=%async_computation.17 | async-start | bytes 1769472 | tf_op jit(solution)/shard_map/all_gather | solution.py:188
  140.0 204.0 %all-gather.23.cloned.1.call-start = ((), (), s32[]{:S(2)}) async-start(), calls=%async_computation.19 | async-start | bytes 2621440 | tf_op jit(solution)/shard_map/all_gather | solution.py:298
  140.7 260.6 %reduce-scatter.16.cloned.1.call-start = ((), (), s32[]{:S(2)}) async-start(), calls=%async_computation.20 | async-start | bytes 2621440 | tf_op jit(solution)/shard_map/reduce_scatter | solution.py:306
  149.5 253.7 %copy-start.47 = (f32[8,1,128]{2,1,0:T(1,128)}, f32[8,1,128]{2,1,0:T(1,128)S(1)}, u32[]{:S(2)}) copy-start(f32[8,1,128]{2,1,0:T(1,128)S(1)} %convert_element_type.102) | copy-start | bytes 12292
  215.3 188.0 %copy-start.10 = (f32[256,1024]{1,0:T(8,128)}, f32[256,1024]{1,0:T(8,128)S(1)}, u32[]{:S(2)}) copy-start(f32[256,1024]{1,0:T(8,128)S(1)} %get-tuple-element.310) | copy-start | bytes 3145732
  215.3 188.0 %copy-start.55 = (f32[256]{0:T(256)}, f32[256]{0:T(256)S(1)}, u32[]{:S(2)}) copy-start(f32[256]{0:T(256)S(1)} %fusion.63) | copy-start | bytes 3076
  215.4 13.4 %collective-permute-start = (bf16[256,1024]{1,0:T(8,128)(2,1)S(1)}, bf16[256,1024]{1,0:T(8,128)(2,1)S(1)}, u32[]{:S(2)}, u32[]{:S(2)}) collective-permute-start(bf16[256,1024]{1,0:T(8,128)(2,1)S(1)} %multiply_convert_fusion.3), channel_id=1, source_target_pairs={{0,1},{1,0},{2,3},{3,2},{4,5},{5,4},{6,7},{7,6},{8,9},{9,8},{10,11... | collective-permute-start | bytes 1572872 | tf_op jit(solution)/shard_map/ppermute | solution.py:249
  230.3 48.2 %collective-permute-start.1 = (bf16[512,1024]{1,0:T(8,128)(2,1)}, bf16[512,1024]{1,0:T(8,128)(2,1)S(1)}, u32[]{:S(2)}, u32[]{:S(2)}) collective-permute-start(bf16[512,1024]{1,0:T(8,128)(2,1)} %maximum_select_fusion.1), channel_id=1, source_target_pairs={{0,2},{1,3},{2,0},{3,1},{4,6},{5,7},{6,4},{7,5},{8,10},{9,11},{10,... | collective-permute-start | bytes 3145736 | tf_op jit(solution)/shard_map/ppermute | solution.py:249
  278.5 9.0 copy-start.70
  343.9 9.6 copy-start.35
  358.6 44.6 %copy-start.24 = (bf16[256,1024]{1,0:T(8,128)(2,1)S(1)}, bf16[256,1024]{1,0:T(8,128)(2,1)}, u32[]{:S(2)}) copy-start(bf16[256,1024]{1,0:T(8,128)(2,1)} %param.31) | copy-start | bytes 1572868
  358.7 91.8 %all-gather.25.cloned.1.call-start = ((), (), s32[]{:S(2)}) async-start(), calls=%async_computation.21 | async-start | bytes 2621440 | tf_op jit(solution)/shard_map/all_gather | solution.py:315
  405.5 192.7 %reduce-scatter.18.cloned.1.call-start = ((), (), s32[]{:S(2)}) async-start(), calls=%async_computation.22 | async-start | bytes 2621440 | tf_op jit(solution)/shard_map/reduce_scatter | solution.py:332
  454.7 9.2 copy-start.3
  457.4 4.1 copy-start
  486.4 4.6 copy-start.1
  486.4 4.7 copy-start.8
  494.7 9.2 copy-start.3
  497.5 4.1 copy-start
  526.5 4.6 copy-start.1
  526.5 4.7 copy-start.8
  531.2 4.7 copy-start.4
  531.2 4.7 copy-start.13
  535.9 4.3 copy-start.23
  535.9 6.6 copy-start.42
  555.5 87.8 %reduce-scatter.14.cloned.1.call-start = ((), (), s32[]{:S(2)}) async-start(), calls=%async_computation.18 | async-start | bytes 2621440 | tf_op jit(solution)/shard_map/reduce_scatter | solution.py:263
  561.5 131.1 %reduce-scatter.28.cloned.1.call-start = ((), (), s32[]{:S(2)}) async-start(), calls=%async_computation.27 | async-start | bytes 3538944 | tf_op jit(solution)/shard_map/reduce_scatter | solution.py:365
  572.1 170.4 %reduce-scatter.30.cloned.1.call-start = ((), (), s32[]{:S(2)}) async-start(), calls=%async_computation.28 | async-start | bytes 3538944 | tf_op jit(solution)/shard_map/reduce_scatter | solution.py:366
  572.7 219.7 %reduce-scatter.32.cloned.1.call-start = ((), (), s32[]{:S(2)}) async-start(), calls=%async_computation.29 | async-start | bytes 3538944 | tf_op jit(solution)/shard_map/reduce_scatter | solution.py:367
  578.7 253.3 %reduce-scatter.22.cloned.1.call-start = ((), (), s32[]{:S(2)}) async-start(), calls=%async_computation.24 | async-start | bytes 1179648 | tf_op jit(solution)/shard_map/reduce_scatter | solution.py:359
  586.5 285.1 %reduce-scatter.24.cloned.1.call-start = ((), (), s32[]{:S(2)}) async-start(), calls=%async_computation.25 | async-start | bytes 1179648 | tf_op jit(solution)/shard_map/reduce_scatter | solution.py:360
  587.1 329.4 %reduce-scatter.26.cloned.1.call-start = ((), (), s32[]{:S(2)}) async-start(), calls=%async_computation.26 | async-start | bytes 2359296 | tf_op jit(solution)/shard_map/reduce_scatter | solution.py:363
  590.8 370.7 %reduce-scatter.20.cloned.1.call-start = ((), (), s32[]{:S(2)}) async-start(), calls=%async_computation.23 | async-start | bytes 2359296 | tf_op jit(solution)/shard_map/reduce_scatter | solution.py:358
  590.8 7.3 copy-start.54
  590.8 7.3 copy-start.59
  593.9 4.2 copy-start.18
  593.9 5.7 copy-start.57
  593.9 31.5 %copy-start.63 = (f32[256]{0:T(256)S(1)}, f32[256]{0:T(256)}, u32[]{:S(2)}) copy-start(f32[256]{0:T(256)} %copy-done.62) | copy-start | bytes 3076
  593.9 49.4 %copy-start.11 = (f32[256,1024]{1,0:T(8,128)S(1)}, f32[256,1024]{1,0:T(8,128)}, u32[]{:S(2)}) copy-start(f32[256,1024]{1,0:T(8,128)} %copy-done.10) | copy-start | bytes 3145732
  594.0 49.4 %copy-start.25 = (bf16[256,1024]{1,0:T(8,128)(2,1)S(1)}, bf16[256,1024]{1,0:T(8,128)(2,1)}, u32[]{:S(2)}) copy-start(bf16[256,1024]{1,0:T(8,128)(2,1)} %param.31) | copy-start | bytes 1572868
  594.0 49.4 %copy-start.26 = (bf16[256,1024]{1,0:T(8,128)(2,1)S(1)}, bf16[256,1024]{1,0:T(8,128)(2,1)}, u32[]{:S(2)}) copy-start(bf16[256,1024]{1,0:T(8,128)(2,1)} %reduce-scatter.16.cloned.1.call-done) | copy-start | bytes 1572868
  594.0 49.4 %copy-start.48 = (f32[8,1,128]{2,1,0:T(1,128)S(1)}, f32[8,1,128]{2,1,0:T(1,128)}, u32[]{:S(2)}) copy-start(f32[8,1,128]{2,1,0:T(1,128)} %copy-done.47) | copy-start | bytes 12292
  594.0 49.4 %copy-start.56 = (f32[256]{0:T(256)S(1)}, f32[256]{0:T(256)}, u32[]{:S(2)}) copy-start(f32[256]{0:T(256)} %copy-done.55) | copy-start | bytes 3076
  594.0 49.4 %copy-start.61 = (f32[256]{0:T(256)S(1)}, f32[256]{0:T(256)}, u32[]{:S(2)}) copy-start(f32[256]{0:T(256)} %copy-done.60) | copy-start | bytes 3076
  (44 other events, 92.4 us)
Sparse Core Ops, SparseCore 0:
  9.9 26.0 all-gather.12
  38.2 45.6 all-gather.10
  85.8 22.2 all-gather.14
  138.2 75.6 reduce-scatter.11
  215.5 26.0 all-gather.16
  243.4 25.5 all-gather.18
  270.9 25.7 all-gather.20
  298.3 45.6 all-gather.22
  358.8 42.4 reduce-scatter.15
  405.6 44.8 all-gather.24
  555.7 42.4 reduce-scatter.17
  600.3 43.0 reduce-scatter.13
  647.3 45.2 reduce-scatter.27
  696.4 46.0 reduce-scatter.29
  746.3 46.0 reduce-scatter.31
  796.0 35.9 reduce-scatter.21
  835.7 35.9 reduce-scatter.23
  875.4 41.0 reduce-scatter.25
  920.4 41.0 reduce-scatter.19
